TPU v7x, 256 devices: a whole 4x4x8 slice. The times are simulated.
256 devices in a mesh: rows: 64 (over z_lo, x, y, core), rep: 4 (over z_hi).
Axes of the slice: x: 4, y: 4, z: 8 (z_hi: 4, z_lo: 2; z = z_hi * 2 + z_lo), core: 2. Of those that a mesh axis runs over, the one named last changes fastest.
Arguments:
- maps: float32 [4, 4096, 4096], P('rep', 'rows'), may hold values from -12 to 12
- mask: int32 [4096, 4096], P('rows'), may hold values 0 or 1
- bins: int32 [4096, 4096], P(None, 'rows'), may hold values from 0 to 1023
Outputs:
- spectra: float32 [2, 3, 1024], replicated
All inputs are finite; a program needn't handle non-finite values. No bound on the sum of `mask` on one device may be relied on, other than what follows from the above.
Results may differ from a plain program's by a relative error of at most 0.0016.
Values sent between devices are 32-bit elements; how exact they have to be, the bound alone decides.
A program may use at most 64 MiB of HBM per device.

v0:
```python
import functools
import math

import jax
import jax.numpy as jnp
import numpy as np
from jax import lax
from jax.experimental import pallas as pl
from jax.experimental.pallas import tpu as pltpu
from jax.sharding import Mesh
from jax.sharding import PartitionSpec as P

NBINS = 1024
SIDE = 4096
MESH = pl.DeviceIdType.MESH
BF = jnp.bfloat16
F32 = jnp.float32
VMEM = pltpu.VMEM
ZSTRIDE = 136


def halves(table):
    high = np.asarray(table, np.float32).astype(BF)
    low = (np.asarray(table, np.float64) - high.astype(np.float64)).astype(np.float32).astype(BF)
    return high, low


def angle(first, second, period):
    return 2.0 * np.pi * ((np.asarray(first)[:, None] * np.asarray(second)[None, :]) % period) / period


def row_tables():
    first = angle(np.arange(32), np.arange(32), 32)
    stage = np.concatenate([np.cos(first), -np.sin(first)], 0)
    first_high, first_low = halves(np.kron(stage, np.eye(8)))
    turn = angle(np.arange(32), np.arange(128), 4096)
    turn_cos = np.repeat(np.cos(turn)[:, None, :], 8, 1).astype(np.float32)
    turn_sin = np.repeat(-np.sin(turn)[:, None, :], 8, 1).astype(np.float32)
    last = angle(np.arange(64), np.arange(128), 128)
    cos, sin = np.cos(last), np.sin(last)
    last_high, last_low = halves(np.block([[cos, sin], [-sin, cos]]))
    alternate = np.zeros((16, 256), np.float32)
    alternate[0, :128] = 1.0 - 2.0 * (np.arange(128) % 2)
    return first_high, first_low, turn_cos, turn_sin, last_high, last_low, alternate.astype(BF)


def column_tables():
    first = angle(np.arange(64), np.arange(64), 64)
    cos, sin = np.cos(first), np.sin(first)
    high, low = halves(np.block([[cos, sin], [-sin, cos]]))
    doubled = np.concatenate([high, high], 1)
    turn = angle(np.arange(64), np.arange(64), 4096)
    turn_cos = np.tile(np.cos(turn), (1, 2)).astype(np.float32)
    turn_sin = np.tile(-np.sin(turn), (1, 2)).astype(np.float32)
    cos2, sin2 = np.kron(np.eye(2), cos), np.kron(np.eye(2), sin)
    last_high, last_low = halves(np.block([[cos2, -sin2], [sin2, cos2]]))
    return doubled, low, turn_cos, turn_sin, last_high, last_low


def split(values):
    high = values.astype(BF)
    return high, (values - high.astype(F32)).astype(BF)


def dot(left, right):
    return jnp.dot(left, right, preferred_element_type=F32)


def dot_nt(left, right):
    return lax.dot_general(left, right, (((1,), (1,)), ((), ())), preferred_element_type=F32)


def slot_of(block):
    group, part = block // 4, block % 4
    return (part % 2) * 64 + (group if part < 2 else 63 - group)


def row_kernel(maps, mask, t1h, t1l, twc, tws, t2h, t2l, alt, out, yh, yl, z):
    for g in range(0, 8, 2):
        pair = []
        for k in (g, g + 1):
            rows = maps[0, 8 * k : 8 * k + 8, :] * mask[8 * k : 8 * k + 8, :].astype(F32)
            pair.append(jnp.concatenate([rows[:, 128 * a : 128 * a + 128] for a in range(32)], 0))
        high, low = split(jnp.concatenate(pair, 1))
        got = dot(t1h[...], high) + dot(t1h[...], low) + dot(t1l[...], high)
        real = got[:256].reshape(32, 8, 256)
        imag = got[256:].reshape(32, 8, 256)
        for k in (0, 1):
            re, im = real[:, :, 128 * k : 128 * k + 128], imag[:, :, 128 * k : 128 * k + 128]
            pair[k] = (re * twc[...] - im * tws[...], re * tws[...] + im * twc[...])
        for part in (0, 1):
            high, low = split(jnp.concatenate([pair[0][part], pair[1][part]], 1))
            yh[:, 8 * g : 8 * g + 16, 128 * part : 128 * part + 128] = high
            yl[:, 8 * g : 8 * g + 16, 128 * part : 128 * part + 128] = low
    for jj in range(8):
        high = yh[4 * jj : 4 * jj + 4].reshape(256, 256)
        low = yl[4 * jj : 4 * jj + 4].reshape(256, 256)
        got = dot_nt(t2h[...], high) + dot_nt(t2h[...], low) + dot_nt(t2l[...], high)
        for k in (0, 1):
            z[ZSTRIDE * (2 * jj + k) : ZSTRIDE * (2 * jj + k) + 128, :] = got[:, 128 * k : 128 * k + 128]
        if jj == 0:
            edge = dot_nt(alt[...], high) + dot_nt(alt[...], low)
            lane = lax.broadcasted_iota(jnp.int32, (8, 128), 1)
            row = lax.broadcasted_iota(jnp.int32, (8, 128), 0)
            old = got[64:72, :128]
            z[64:72, :] = jnp.where((row == 0) & (lane < 64), edge[0:8, :128], old)
    for block in range(128):
        q2, h = block // 2, block % 2
        for ri in (0, 1):
            start = ZSTRIDE * 8 * h + 64 * ri + q2
            out[slot_of(block), 8 * ri : 8 * ri + 8, :] = z[pl.ds(start, 8, stride=ZSTRIDE), :]


def row_blocks(maps, mask):
    return pl.pallas_call(
        row_kernel,
        out_shape=jax.ShapeDtypeStruct((128, 16, 128), F32),
        in_specs=[pl.BlockSpec(memory_space=VMEM)] * 9,
        out_specs=pl.BlockSpec(memory_space=VMEM),
        scratch_shapes=[VMEM((32, 64, 256), BF), VMEM((32, 64, 256), BF), VMEM((16 * ZSTRIDE, 128), F32)],
        compiler_params=pltpu.CompilerParams(vmem_limit_bytes=40 << 20),
        name="row_dft",
    )(maps, mask, *row_tables())


def exchange_kernel(x, o, send_sem, recv_sem):
    r, s, m = lax.axis_index("rows"), lax.axis_index("sky"), lax.axis_index("pair")
    me = m * 64 + r

    def target(i):
        t = lax.rem(me + i, 128)
        return t, {"rows": lax.rem(t, 64), "sky": s, "pair": t // 64}

    barrier = pltpu.get_barrier_semaphore()

    def greet(i, carry):
        _, where = target(i)
        pl.semaphore_signal(barrier, inc=1, device_id=where, device_id_type=MESH)
        return carry

    lax.fori_loop(1, 128, greet, 0)
    pl.semaphore_wait(barrier, 127)

    def send(i, carry):
        t, where = target(i)
        pltpu.make_async_remote_copy(
            src_ref=x.at[t], dst_ref=o.at[me], send_sem=send_sem, recv_sem=recv_sem,
            device_id=where, device_id_type=MESH,
        ).start()
        return carry

    lax.fori_loop(1, 128, send, 0)
    o[me] = x[me]
    pltpu.make_async_copy(x.at[pl.ds(0, 127)], o.at[pl.ds(0, 127)], send_sem).wait()
    pltpu.make_async_copy(x.at[pl.ds(0, 127)], o.at[pl.ds(0, 127)], recv_sem).wait()


def exchange(blocks):
    return pl.pallas_call(
        exchange_kernel,
        out_shape=jax.ShapeDtypeStruct(blocks.shape, blocks.dtype),
        in_specs=[pl.BlockSpec(memory_space=VMEM)],
        out_specs=pl.BlockSpec(memory_space=VMEM),
        scratch_shapes=[pltpu.SemaphoreType.DMA, pltpu.SemaphoreType.DMA],
        compiler_params=pltpu.CompilerParams(collective_id=0, has_side_effects=True),
        name="sky_exchange",
    )(blocks)


def bins_kernel(bins, own, send, first, scr):
    r, m = lax.axis_index("rows"), lax.axis_index("pair")
    upper = (r >= 32).astype(jnp.int32)
    scr[0:4096, :] = bins[...].astype(F32)
    scr[4096:4104, :] = bins[0:8, :].astype(F32)
    row = lax.broadcasted_iota(jnp.int32, (48, 64), 0)
    col = lax.broadcasted_iota(jnp.int32, (48, 64), 1)
    offset = 2 * (row % 8) + (row // 8) % 2
    sent = row // 16
    below = 16 * m + 32 * sent + offset
    above = 32 + 32 * sent - 16 * m - offset
    wanted = jnp.where(row >= 32, jnp.where(row == 32, 0, -1), jnp.where(upper == 1, above, below))
    pick = (wanted == col).astype(F32)
    pick_high, pick_low = (32.0 * pick).astype(BF), pick.astype(BF)
    src = lax.broadcasted_iota(jnp.int32, (64, 128), 0)
    lane = lax.broadcasted_iota(jnp.int32, (64, 128), 1)
    there = jnp.where(upper == 1, 63 - src, src)
    put = [(lane == there + 64 * half).astype(F32) for half in (0, 1)]
    put_high = [(32.0 * one).astype(BF) for one in put]
    put_low = [one.astype(BF) for one in put]

    def body(k, carry):
        for u in range(4):
            p1 = 4 * k + u
            start = jnp.where(upper == 1, 64 - p1, p1)
            block = scr[pl.ds(start, 64, stride=64), :]
            high = jnp.floor(block * (1.0 / 32.0))
            low = block - 32.0 * high
            got = dot_nt(pick_high, high.astype(BF)) + dot_nt(pick_low, low.astype(BF))
            high = jnp.floor(got * (1.0 / 32.0))
            low = (got - 32.0 * high).astype(BF)
            high = high.astype(BF)
            wide = [dot(high, put_high[i]) + dot(low, put_low[i]) for i in (0, 1)]
            own[pl.ds(p1, 8, stride=64), :] = wide[0][0:8] + wide[1][8:16]
            send[pl.ds(p1, 8, stride=64), :] = wide[0][16:24] + wide[1][24:32]
            first[pl.ds(p1, 1), :] = wide[0][32:33] + wide[1][32:33]
        return carry

    lax.fori_loop(0, 16, body, 0)


def arrange_bins(bins):
    return pl.pallas_call(
        bins_kernel,
        out_shape=[
            jax.ShapeDtypeStruct((512, 128), F32),
            jax.ShapeDtypeStruct((512, 128), F32),
            jax.ShapeDtypeStruct((64, 128), F32),
        ],
        in_specs=[pl.BlockSpec(memory_space=VMEM)],
        out_specs=[pl.BlockSpec(memory_space=VMEM)] * 3,
        scratch_shapes=[VMEM((4104, 64), F32)],
        compiler_params=pltpu.CompilerParams(vmem_limit_bytes=30 << 20),
        name="bin_layout",
    )(bins)


def column_kernel(got, own, other, first, tah, tal, twc, tws, t2h, t2l, out, powers, index):
    r, m = lax.axis_index("rows"), lax.axis_index("pair")
    lower = r < 32
    block = jnp.where(lower, 4 * r + m, 4 * (63 - r) + 2 + m)
    p1 = lax.broadcasted_iota(jnp.int32, (64, 128), 0)
    lane = lax.broadcasted_iota(jnp.int32, (64, 128), 1)
    p = p1 + 64 * (lane % 64)
    second = lane // 64
    signed = jnp.where(p >= SIDE // 2, p - SIDE, p)
    back = jnp.where(p == SIDE // 2, signed, -signed)
    zero = jnp.zeros((64, 128), F32)
    out[...] = jnp.zeros_like(out)

    def spectrum(parts):
        high, low = split(jnp.concatenate([jnp.concatenate(part, 0) for part in parts], 1))
        mid = dot(tah[...], jnp.concatenate([high, low], 0)) + dot(tal[...], high)
        turned = []
        for k in (0, 1):
            re, im = mid[:64, 128 * k : 128 * k + 128], mid[64:, 128 * k : 128 * k + 128]
            turned.append(
                jnp.concatenate([re * twc[...] - im * tws[...], re * tws[...] + im * twc[...]], 1)
            )
        high, low = split(jnp.concatenate(turned, 0))
        last = dot(high, t2h[...]) + dot(low, t2h[...]) + dot(high, t2l[...])
        return last[:64, :128], last[:64, 128:], last[64:, :128], last[64:, 128:]

    def set_powers(base, fields, cos_twice, sin_twice):
        q_re, q_im, u_re, u_im = fields
        e_re = cos_twice * q_re + sin_twice * u_re
        e_im = cos_twice * q_im + sin_twice * u_im
        b_re = cos_twice * u_re - sin_twice * q_re
        b_im = cos_twice * u_im - sin_twice * q_im
        scale = 1.0 / (SIDE * SIDE)
        terms = (e_re * e_re + e_im * e_im, b_re * b_re + b_im * b_im, e_re * b_re + e_im * b_im)
        for k in range(3):
            powers[base + k] = (terms[k] * scale).astype(BF).astype(F32)

    def turn(freq_x, freq_y):
        radius = jnp.maximum(freq_x * freq_x + freq_y * freq_y, 1.0)
        return (freq_x * freq_x - freq_y * freq_y) / radius, 2.0 * freq_x * freq_y / radius

    def set_index(base, values):
        high = jnp.floor(values * (1.0 / 32.0))
        index[base] = high
        index[base + 1] = values - 32.0 * high

    want = lax.broadcasted_iota(jnp.int32, (32, 128), 0).astype(F32)
    one = jnp.ones((32, 128), F32)
    none = jnp.zeros((32, 128), F32)

    def add_up(kind):
        def body(k, carry):
            base = pl.multiple_of(8 * k, 8)
            hi, lo = index[2 * kind, pl.ds(base, 8), :], index[2 * kind + 1, pl.ds(base, 8), :]
            vals = [powers[3 * kind + c, pl.ds(base, 8), :] for c in range(3)]
            left, right = [], []
            for i in range(8):
                hot = jnp.broadcast_to(hi[i : i + 1], (32, 128)) == want
                cols = [
                    jnp.where(hot, jnp.broadcast_to(vals[c][i : i + 1], (32, 128)), none) for c in range(3)
                ]
                left.append(jnp.concatenate(cols, 0).astype(BF))
                right.append(
                    jnp.where(jnp.broadcast_to(lo[i : i + 1], (32, 128)) == want, one, none).astype(BF)
                )
            return carry + dot_nt(jnp.concatenate(left, 1), jnp.concatenate(right, 1))

        out[...] += lax.fori_loop(0, 8, body, jnp.zeros((96, 32), F32))

    def pair_of(j):
        parts = []
        for k in (0, 1):
            parts.append(
                [got[pl.ds(1024 * k + 8 * c + j, 64, stride=16), :] for c in (0, 1)]
            )
        return parts

    def columns(j, carry):
        fields = spectrum(pair_of(j))
        freq_x = (16 * block + 2 * j + second).astype(F32)
        cos_twice, sin_twice = turn(freq_x, signed.astype(F32))
        set_powers(0, fields, cos_twice, sin_twice)
        set_powers(3, fields, cos_twice, jnp.where(p == SIDE // 2, -sin_twice, sin_twice))
        rows = pl.ds(pl.multiple_of(64 * j, 64), 64)
        mine, theirs = own[rows, :], other[rows, :]
        ahead = jnp.where(lower, mine, theirs)
        mirror = jnp.where(lower, theirs, mine)
        edge = (j == 0) & lower & (m == 0)
        mirror = jnp.where(edge & (second == 0), first[...], mirror)
        packed = edge & (r == 0) & (second == 0)
        set_index(0, jnp.where(packed, -1.0, ahead))
        set_index(2, jnp.where(packed, -1.0, mirror))
        add_up(0)
        add_up(1)
        return carry

    lax.fori_loop(0, 8, columns, 0)

    parts = []
    for re, im in pair_of(0):
        parts.append([jnp.where(second == 0, re, pltpu.roll(im, 64, 1)), zero])
    fields = spectrum(parts)
    freq_x = jnp.where(second == 0, 0.0, -(SIDE // 2) * 1.0)
    freq_y = jnp.where(second == 0, signed, back).astype(F32)
    set_powers(0, fields, *turn(freq_x, freq_y))
    special = jnp.where(second == 0, own[0:64, :], first[...])
    set_index(0, jnp.where((r == 0) & (m == 0), special, -1.0))
    add_up(0)


def binned(blocks, own, other, first):
    return pl.pallas_call(
        column_kernel,
        out_shape=jax.ShapeDtypeStruct((96, 32), F32),
        in_specs=[pl.BlockSpec(memory_space=VMEM)] * 10,
        out_specs=pl.BlockSpec(memory_space=VMEM),
        scratch_shapes=[VMEM((6, 64, 128), F32), VMEM((4, 64, 128), F32)],
        compiler_params=pltpu.CompilerParams(vmem_limit_bytes=40 << 20),
        name="column_bins",
    )(blocks.reshape(2048, 128), own, other, first, *column_tables())


def total_kernel(part, out, stage, seen_a, seen_b, seen_c, send_sem, recv_sem):
    r, s, m = lax.axis_index("rows"), lax.axis_index("sky"), lax.axis_index("pair")
    low, high = lax.rem(r, 8), r // 8
    rep = 2 * s + m
    peers = [[], [], []]
    for i in range(1, 8):
        peers[0].append({"rows": high * 8 + lax.rem(low + i, 8), "sky": s, "pair": m})
        peers[1].append({"rows": lax.rem(high + i, 8) * 8 + low, "sky": s, "pair": m})
    for i in range(1, 4):
        other = lax.rem(rep + i, 4)
        peers[2].append({"rows": r, "sky": other // 2, "pair": lax.rem(other, 2)})
    barrier = pltpu.get_barrier_semaphore()
    for group in peers:
        for where in group:
            pl.semaphore_signal(barrier, inc=1, device_id=where, device_id_type=MESH)
    pl.semaphore_wait(barrier, 17)

    def phase(k, src, seen, me):
        count = len(peers[k])
        for where in peers[k]:
            pltpu.make_async_remote_copy(
                src_ref=src, dst_ref=seen.at[me], send_sem=send_sem.at[k], recv_sem=recv_sem.at[k],
                device_id=where, device_id_type=MESH,
            ).start()
        seen[me] = src[...]
        whole = seen.at[pl.ds(0, count)]
        pltpu.make_async_copy(whole, whole, send_sem.at[k]).wait()
        pltpu.make_async_copy(whole, whole, recv_sem.at[k]).wait()

    phase(0, part, seen_a, low)
    stage[0] = jnp.sum(seen_a[...], axis=0)
    phase(1, stage.at[0], seen_b, high)
    stage[1] = jnp.sum(seen_b[...], axis=0)
    phase(2, stage.at[1], seen_c, rep)
    auto = NBINS / (SIDE * SIDE)
    row = lax.broadcasted_iota(jnp.int32, (24, 128), 0)
    factors = jnp.where(row < 16, auto, math.sqrt(auto))
    for sky in (0, 1):
        out[sky] = (seen_c[2 * sky] + seen_c[2 * sky + 1]) * factors


def totals(part):
    return pl.pallas_call(
        total_kernel,
        out_shape=jax.ShapeDtypeStruct((2, 24, 128), F32),
        in_specs=[pl.BlockSpec(memory_space=VMEM)],
        out_specs=pl.BlockSpec(memory_space=VMEM),
        scratch_shapes=[
            VMEM((2, 24, 128), F32),
            VMEM((8, 24, 128), F32),
            VMEM((8, 24, 128), F32),
            VMEM((4, 24, 128), F32),
            pltpu.SemaphoreType.DMA((3,)),
            pltpu.SemaphoreType.DMA((3,)),
        ],
        compiler_params=pltpu.CompilerParams(collective_id=1, has_side_effects=True),
        name="sky_totals",
    )(part)


def on_device(maps, mask, bins):
    own, send, first = arrange_bins(bins)
    other = lax.ppermute(send, "rows", [(i, 63 - i) for i in range(64)])
    column = lax.ppermute(first, "rows", [(32, 0)] + [(i, 64 - i) for i in range(33, 64)])
    blocks = exchange(row_blocks(maps, mask))
    part = binned(blocks, own, other, column)
    return totals(part.reshape(24, 128)).reshape(2, 3, NBINS)


def solution(mesh):
    parted = Mesh(mesh.devices.reshape(mesh.shape["rows"], 2, 2), ("rows", "sky", "pair"))
    placed = (P(("sky", "pair"), "rows", None), P("rows", None), P(None, "rows"))
    return jax.shard_map(on_device, mesh=parted, in_specs=placed, out_specs=P(), check_vma=False)
```

profile of v0, /device:TPU:1, one launch (start us, length us, event | category | flops | bytes accessed | tf_op | source)
XLA Modules:
  0.0 113.1 jit_solution(9441059960157435118)
XLA Ops:
  0.0 0.0 copy-start.4
  0.0 0.0 copy-start.10
  0.0 0.0 copy-start.18
  0.0 0.0 copy-start.2
  0.0 1.9 %copy.19.bins = s32[4096,64]{1,0:T(8,128)S(1)} copy(s32[4096,64]{0,1:T(8,128)} %param.18) | data formatting | bytes 2097152 | tf_op args[2]
  2.0 0.0 copy-start.3
  2.0 0.0 copy-start.5
  2.0 0.0 copy-start.11
  2.0 0.0 copy-start.12
  2.0 0.0 copy-start.13
  2.0 8.3 %bin_layout.1 = (f32[512,128]{1,0:T(8,128)S(1)}, f32[512,128]{1,0:T(8,128)}, f32[64,128]{1,0:T(8,128)}) custom-call(s32[4096,64]{1,0:T(8,128)S(1)} %copy.19.bins), custom_call_target="tpu_custom_call" | custom-call | tf_op jit(solution)/shard_map/bin_layout/pallas_call | solution.py:212
  10.4 0.0 copy-start.6
  10.4 0.7 copy-done.6
  11.1 7.7 %collective-permute-start = (f32[512,128]{1,0:T(8,128)}, f32[512,128]{1,0:T(8,128)S(1)}, u32[]{:S(2)}, u32[]{:S(2)}) collective-permute-start(f32[512,128]{1,0:T(8,128)} %get-tuple-element.9), channel_id=1, source_target_pairs={{0,252},{4,248},{8,244},{12,240},{16,236},{20,232},{24,228},{28,22... | collective-permute-start | bytes 786440 | tf_op jit(solution)/shard_map/ppermute | solution.py:411
  18.7 0.0 copy-start.7
  18.7 0.0 copy-start.15
  18.7 0.0 copy-start.16
  18.8 0.0 copy-start.17
  18.8 1.4 %collective-permute-start.1 = (f32[64,128]{1,0:T(8,128)}, f32[64,128]{1,0:T(8,128)S(1)}, u32[]{:S(2)}, u32[]{:S(2)}) collective-permute-start(f32[64,128]{1,0:T(8,128)} %get-tuple-element.10), channel_id=1, source_target_pairs={{128,0},{132,124},{136,120},{140,116},{144,112},{148,108},{152,104... | collective-permute-start | bytes 98312 | tf_op jit(solution)/shard_map/ppermute | solution.py:412
  20.2 0.0 copy-done.4
  20.2 0.0 copy-done.10
  20.2 0.0 copy-done.18
  20.2 0.0 copy-done.2
  20.2 0.0 copy-done.3
  20.3 0.0 copy-done.5
  20.3 0.0 copy-done.11
  20.3 0.0 copy-done.12
  20.3 0.0 copy-done.13
  20.3 2.5 %row_dft.1.x = f32[128,16,128]{2,1,0:T(8,128)S(1)} custom-call(f32[1,64,4096]{2,1,0:T(8,128)S(1)} %copy-done.2, s32[64,4096]{1,0:T(8,128)S(1)} %copy-done.3, bf16[512,256]{1,0:T(8,128)(2,1)S(1)} %copy-done.4, bf16[512,256]{1,0:T(8,128)(2,1)S(1)} %copy-done.5, f32[32,8,128]{2,1,0:T(8,128)S(1)} %copy-done.10, f32[32,8,128]{2,1,0:T(8,128)S(1)} %copy-done.11, ...), custom_call_target="tpu_custom_call" | custom-call | tf_op jit(solution)/shard_map/row_dft/pallas_call | solution.py:115
  22.8 0.0 copy-start.1
  22.8 1.0 copy-done.1
  23.7 28.3 %sky_exchange.1 = f32[128,16,128]{2,1,0:T(8,128)} custom-call(f32[128,16,128]{2,1,0:T(8,128)} %copy-done.1), custom_call_target="tpu_custom_call" | custom-call | tf_op jit(solution)/shard_map/sky_exchange/pallas_call | solution.py:159
  52.1 0.0 collective-permute-done.1.first
  52.1 0.0 collective-permute-done.other
  52.1 0.0 copy-done.7
  52.1 0.0 copy-done.8
  52.1 0.0 copy-done.9
  52.1 0.0 copy-done.14
  52.1 0.0 copy-done.15
  52.2 0.0 copy-done.16
  52.2 0.0 copy-done.17
  52.2 0.0 copy-start
  52.2 1.2 %copy-done = f32[128,16,128]{2,1,0:T(8,128)S(1)} copy-done((f32[128,16,128]{2,1,0:T(8,128)S(1)}, f32[128,16,128]{2,1,0:T(8,128)}, u32[]{:S(2)}) %copy-start) | copy-done | bytes 1048600
  53.4 30.3 %column_bins.1 = f32[96,32]{1,0:T(8,128)S(1)} custom-call(f32[2048,128]{1,0:T(8,128)S(1)} %bitcast.1, f32[512,128]{1,0:T(8,128)S(1)} %copy-done.7, f32[512,128]{1,0:T(8,128)S(1)} %collective-permute-done.other, f32[64,128]{1,0:T(8,128)S(1)} %collective-permute-done.1.first, bf16[128,256]{1,0:T(8,128)(2,1)S(1)} %copy-done.14, ...), custom_call_target="tpu_custom_call" | custom-call | tf_op jit(solution)/shard_map/column_bins/pallas_call | solution.py:338
  83.7 0.7 reshape.10.part
  84.3 27.3 %sky_totals.1 = f32[2,24,128]{2,1,0:T(8,128)} custom-call(f32[24,128]{1,0:T(8,128)} %reshape.10.part), custom_call_target="tpu_custom_call" | custom-call | tf_op jit(solution)/shard_map/sky_totals/pallas_call | solution.py:391
  111.7 0.8 reshape.11
  112.4 0.6 copy.20
  (3 shorter events, 0.0 us)
Async XLA Ops:
  0.0 20.2 %copy-start.4 = (bf16[512,256]{1,0:T(8,128)(2,1)S(1)}, bf16[512,256]{1,0:T(8,128)(2,1)}, u32[]{:S(2)}) copy-start(bf16[512,256]{1,0:T(8,128)(2,1)} %constant.26.clone.t1h) | copy-start | bytes 786436
  0.0 20.2 %copy-start.10 = (f32[32,8,128]{2,1,0:T(8,128)S(1)}, f32[32,8,128]{2,1,0:T(8,128)}, u32[]{:S(2)}) copy-start(f32[32,8,128]{2,1,0:T(8,128)} %constant.28.clone.twc) | copy-start | bytes 393220
  0.0 20.2 %copy-start.18 = (bf16[16,256]{1,0:T(8,128)(2,1)S(1)}, bf16[16,256]{1,0:T(8,128)(2,1)}, u32[]{:S(2)}) copy-start(bf16[16,256]{1,0:T(8,128)(2,1)} %constant.32.clone.alt) | copy-start | bytes 24580
  0.0 20.2 %copy-start.2 = (f32[1,64,4096]{2,1,0:T(8,128)S(1)}, f32[1,64,4096]{2,1,0:T(8,128)}, u32[]{:S(2)}) copy-start(f32[1,64,4096]{2,1,0:T(8,128)} %maps.1) | copy-start | bytes 3145732
  2.0 18.3 %copy-start.3 = (s32[64,4096]{1,0:T(8,128)S(1)}, s32[64,4096]{1,0:T(8,128)}, u32[]{:S(2)}) copy-start(s32[64,4096]{1,0:T(8,128)} %mask.1) | copy-start | bytes 3145732
  2.0 18.3 %copy-start.5 = (bf16[512,256]{1,0:T(8,128)(2,1)S(1)}, bf16[512,256]{1,0:T(8,128)(2,1)}, u32[]{:S(2)}) copy-start(bf16[512,256]{1,0:T(8,128)(2,1)} %constant.27.clone.t1l) | copy-start | bytes 786436
  2.0 18.3 %copy-start.11 = (f32[32,8,128]{2,1,0:T(8,128)S(1)}, f32[32,8,128]{2,1,0:T(8,128)}, u32[]{:S(2)}) copy-start(f32[32,8,128]{2,1,0:T(8,128)} %constant.29.clone.tws) | copy-start | bytes 393220
  2.0 18.3 %copy-start.12 = (bf16[128,256]{1,0:T(8,128)(2,1)S(1)}, bf16[128,256]{1,0:T(8,128)(2,1)}, u32[]{:S(2)}) copy-start(bf16[128,256]{1,0:T(8,128)(2,1)} %constant.30.clone.t2h) | copy-start | bytes 196612
  2.0 18.3 %copy-start.13 = (bf16[128,256]{1,0:T(8,128)(2,1)S(1)}, bf16[128,256]{1,0:T(8,128)(2,1)}, u32[]{:S(2)}) copy-start(bf16[128,256]{1,0:T(8,128)(2,1)} %constant.31.clone.t2l) | copy-start | bytes 196612
  10.4 0.7 copy-start.6
  11.1 41.0 %collective-permute-start = (f32[512,128]{1,0:T(8,128)}, f32[512,128]{1,0:T(8,128)S(1)}, u32[]{:S(2)}, u32[]{:S(2)}) collective-permute-start(f32[512,128]{1,0:T(8,128)} %get-tuple-element.9), channel_id=1, source_target_pairs={{0,252},{4,248},{8,244},{12,240},{16,236},{20,232},{24,228},{28,22... | collective-permute-start | bytes 786440 | tf_op jit(solution)/shard_map/ppermute | solution.py:411
  18.7 33.4 %copy-start.7 = (f32[512,128]{1,0:T(8,128)S(1)}, f32[512,128]{1,0:T(8,128)}, u32[]{:S(2)}) copy-start(f32[512,128]{1,0:T(8,128)} %copy-done.6) | copy-start | bytes 786436
  18.7 33.4 %copy-start.8 = (bf16[256,256]{1,0:T(8,128)(2,1)S(1)}, bf16[256,256]{1,0:T(8,128)(2,1)}, u32[]{:S(2)}) copy-start(bf16[256,256]{1,0:T(8,128)(2,1)} %constant.37.clone.t2h) | copy-start | bytes 393220
  18.7 33.4 %copy-start.9 = (bf16[256,256]{1,0:T(8,128)(2,1)S(1)}, bf16[256,256]{1,0:T(8,128)(2,1)}, u32[]{:S(2)}) copy-start(bf16[256,256]{1,0:T(8,128)(2,1)} %constant.38.clone.t2l) | copy-start | bytes 393220
  18.7 33.4 %copy-start.14 = (bf16[128,256]{1,0:T(8,128)(2,1)S(1)}, bf16[128,256]{1,0:T(8,128)(2,1)}, u32[]{:S(2)}) copy-start(bf16[128,256]{1,0:T(8,128)(2,1)} %constant.33.clone.tah) | copy-start | bytes 196612
  18.7 33.4 %copy-start.15 = (bf16[128,128]{1,0:T(8,128)(2,1)S(1)}, bf16[128,128]{1,0:T(8,128)(2,1)}, u32[]{:S(2)}) copy-start(bf16[128,128]{1,0:T(8,128)(2,1)} %constant.34.clone.tal) | copy-start | bytes 98308
  18.7 33.4 %copy-start.16 = (f32[64,128]{1,0:T(8,128)S(1)}, f32[64,128]{1,0:T(8,128)}, u32[]{:S(2)}) copy-start(f32[64,128]{1,0:T(8,128)} %constant.35.clone.twc) | copy-start | bytes 98308
  18.8 33.4 %copy-start.17 = (f32[64,128]{1,0:T(8,128)S(1)}, f32[64,128]{1,0:T(8,128)}, u32[]{:S(2)}) copy-start(f32[64,128]{1,0:T(8,128)} %constant.36.clone.tws) | copy-start | bytes 98308
  18.8 33.3 %collective-permute-start.1 = (f32[64,128]{1,0:T(8,128)}, f32[64,128]{1,0:T(8,128)S(1)}, u32[]{:S(2)}, u32[]{:S(2)}) collective-permute-start(f32[64,128]{1,0:T(8,128)} %get-tuple-element.10), channel_id=1, source_target_pairs={{128,0},{132,124},{136,120},{140,116},{144,112},{148,108},{152,104... | collective-permute-start | bytes 98312 | tf_op jit(solution)/shard_map/ppermute | solution.py:412
  22.8 1.0 copy-start.1
  52.2 1.2 %copy-start = (f32[128,16,128]{2,1,0:T(8,128)S(1)}, f32[128,16,128]{2,1,0:T(8,128)}, u32[]{:S(2)}) copy-start(f32[128,16,128]{2,1,0:T(8,128)} %sky_exchange.1) | copy-start | bytes 3145732
where the time goes:
time: 113 us
  Pallas kernels  96.7 us (86%)
  starting transfers between devices  9.08 us (8%)
  local copies, waits for them, and re-layouts  6.96 us (6%)
    pallas_call x1, Pallas kernels, binned(): pl.pallas_call(column_kernel, out_shape=jax.ShapeDtypeStruct((96, 32), F3...  30.3 us
    pallas_call x1, Pallas kernels, exchange(): pl.pallas_call(exchange_kernel, out_shape=jax.ShapeDtypeStruct(blocks.sha...  28.3 us
    pallas_call x1, Pallas kernels, totals(): pl.pallas_call(total_kernel, out_shape=jax.ShapeDtypeStruct((2, 24, 128),...  27.3 us
    pallas_call x1, Pallas kernels, arrange_bins(): pl.pallas_call(bins_kernel, out_shape=[jax.ShapeDtypeStruct((512, 128), F...  8.34 us
    ppermute x1, starting transfers between devices, on_device(): other = lax.ppermute(send, 'rows', [(i, 63 - i) for i in range(64)])  7.66 us
    unnamed x39, local copies, waits for them, and re-layouts  4.9 us
    pallas_call x1, Pallas kernels, row_blocks(): pl.pallas_call(row_kernel, out_shape=jax.ShapeDtypeStruct((128, 16, 128),...  2.47 us
  transfers between devices with their start and end apart: 2, of which 0 were waited for; matrix products, arithmetic and copies ran while one was open for 0% of the time, Pallas kernels for 27%

commit v1 on v0

v1 whole, which is shorter than its diff:
```python
import functools
import math

import jax
import jax.numpy as jnp
import numpy as np
from jax import lax
from jax.experimental import pallas as pl
from jax.experimental.pallas import tpu as pltpu
from jax.sharding import Mesh
from jax.sharding import PartitionSpec as P

NBINS = 1024
SIDE = 4096
MESH = pl.DeviceIdType.MESH
BF = jnp.bfloat16
F32 = jnp.float32
VMEM = pltpu.VMEM
STEP = 72
CHUNKS = 2
PAIRS = 8 // CHUNKS
LINES = 2 * PAIRS
UNROLL = 64


def halves(table):
    high = np.asarray(table, np.float32).astype(BF)
    low = (np.asarray(table, np.float64) - high.astype(np.float64)).astype(np.float32).astype(BF)
    return high, low


def angle(first, second, period):
    return 2.0 * np.pi * ((np.asarray(first)[:, None] * np.asarray(second)[None, :]) % period) / period


def row_tables():
    first = angle(np.arange(32), np.arange(32), 32)
    stage = np.concatenate([np.cos(first), -np.sin(first)], 0)
    first_high, first_low = halves(np.kron(stage, np.eye(8)))
    turn = angle(np.arange(32), np.arange(128), 4096)
    turn_cos = np.repeat(np.cos(turn)[:, None, :], 8, 1).astype(np.float32)
    turn_sin = np.repeat(-np.sin(turn)[:, None, :], 8, 1).astype(np.float32)
    last = angle(np.arange(64), np.arange(128), 128)
    cos, sin = np.cos(last), np.sin(last)
    last_high, last_low = halves(np.block([[cos, sin], [-sin, cos]]))
    alternate = np.zeros((16, 256), np.float32)
    alternate[0, :128] = 1.0 - 2.0 * (np.arange(128) % 2)
    return first_high, first_low, turn_cos, turn_sin, last_high, last_low, alternate.astype(BF)


def column_tables():
    first = angle(np.arange(64), np.arange(64), 64)
    cos, sin = np.cos(first), np.sin(first)
    high, low = halves(np.block([[cos, sin], [-sin, cos]]))
    doubled = np.concatenate([high, high], 1)
    turn = angle(np.arange(128), np.arange(64), 4096)
    turn_cos = np.tile(np.cos(turn), (1, 2)).astype(np.float32)
    turn_sin = np.tile(-np.sin(turn), (1, 2)).astype(np.float32)
    last = angle(np.arange(32), np.arange(64), 32)
    cos, sin = np.cos(last), np.sin(last)
    none = np.zeros_like(cos)
    last_high, last_low = halves(
        np.block(
            [
                [cos, none, sin, none],
                [-sin, none, cos, none],
                [none, cos, none, sin],
                [none, -sin, none, cos],
            ]
        )
    )
    flip = np.zeros((128, 128), np.float32)
    flip[(128 - np.arange(128)) % 128, np.arange(128)] = 1.0
    return doubled, low, turn_cos, turn_sin, last_high, last_low, flip.astype(BF)


def split(values):
    high = values.astype(BF)
    return high, (values - high.astype(F32)).astype(BF)


def dot(left, right):
    return jnp.dot(left, right, preferred_element_type=F32)


def dot_nt(left, right):
    return lax.dot_general(left, right, (((1,), (1,)), ((), ())), preferred_element_type=F32)


def slot_of(block):
    group, part = block // 4, block % 4
    return (part % 2) * 64 + (group if part < 2 else 63 - group)


def spread(line):
    tile = jnp.broadcast_to(line, (8, 128))
    return jnp.concatenate([tile, tile], 0).astype(BF)


def kernel(
    maps, mask, bins, t1h, t1l, twc, tws, t2h, t2l, alt, tah, tal, cwc, cws, tbh, tbl, flip,
    out,
    yh, yl, z, x, o, ahead, mirror, ahead_hi, ahead_lo, mirror_hi, mirror_lo, powers, acc,
    stage, seen_a, seen_b, seen_c, send_sem, recv_sem, bin_send, bin_recv, bin_here, sum_send, sum_recv,
):
    r, s, m = lax.axis_index("rows"), lax.axis_index("sky"), lax.axis_index("pair")
    me = m * 64 + r
    lower = r < 32
    low_row, high_row = lax.rem(r, 8), r // 8
    rep = 2 * s + m

    def target(i):
        t = lax.rem(me + i, 128)
        return t, {"rows": lax.rem(t, 64), "sky": s, "pair": t // 64}

    barrier = pltpu.get_barrier_semaphore()

    def greet(i, carry):
        _, where = target(i)
        pl.semaphore_signal(barrier, inc=1, device_id=where, device_id_type=MESH)
        return carry

    lax.fori_loop(1, 128, greet, 0)
    for pair in (0, 1):
        pl.semaphore_signal(
            barrier, inc=1, device_id={"rows": r, "sky": 1 - s, "pair": pair}, device_id_type=MESH
        )

    @pl.when(lower)
    def _():
        pltpu.make_async_copy(bins.at[pl.ds(16 * m, 16)], ahead, bin_here).start()

    @pl.when(jnp.logical_not(lower))
    def _():
        pltpu.make_async_copy(bins.at[pl.ds(16 - 16 * m, 16)], mirror.at[pl.ds(0, 16)], bin_here).start()
        pltpu.make_async_copy(bins.at[pl.ds(32 - 16 * m, 8)], mirror.at[pl.ds(16, 8)], bin_here).start()

    for g in range(0, 8, 2):
        pair = []
        for k in (g, g + 1):
            rows = maps[0, 8 * k : 8 * k + 8, :] * mask[8 * k : 8 * k + 8, :].astype(F32)
            pair.append(jnp.concatenate([rows[:, 128 * a : 128 * a + 128] for a in range(32)], 0))
        high, low = split(jnp.concatenate(pair, 1))
        got = dot(t1h[...], high) + dot(t1h[...], low) + dot(t1l[...], high)
        real = got[:256].reshape(32, 8, 256)
        imag = got[256:].reshape(32, 8, 256)
        for k in (0, 1):
            re, im = real[:, :, 128 * k : 128 * k + 128], imag[:, :, 128 * k : 128 * k + 128]
            pair[k] = (re * twc[...] - im * tws[...], re * tws[...] + im * twc[...])
        for part in (0, 1):
            high, low = split(jnp.concatenate([pair[0][part], pair[1][part]], 1))
            yh[:, 8 * g : 8 * g + 16, 128 * part : 128 * part + 128] = high
            yl[:, 8 * g : 8 * g + 16, 128 * part : 128 * part + 128] = low

    def second_stage(jj):
        high = yh[4 * jj : 4 * jj + 4].reshape(256, 256)
        low = yl[4 * jj : 4 * jj + 4].reshape(256, 256)
        got = dot_nt(t2h[...], high) + dot_nt(t2h[...], low) + dot_nt(t2l[...], high)
        for k in (0, 1):
            for ri in (0, 1):
                start = STEP * (2 * (2 * jj + k) + ri)
                z[start : start + 64, :] = got[64 * ri : 64 * ri + 64, 128 * k : 128 * k + 128]
        if jj == 0:
            edge = dot_nt(alt[...], high) + dot_nt(alt[...], low)
            lane = lax.broadcasted_iota(jnp.int32, (8, 128), 1)
            row = lax.broadcasted_iota(jnp.int32, (8, 128), 0)
            z[STEP : STEP + 8, :] = jnp.where((row == 0) & (lane < 64), edge[0:8, :128], got[64:72, :128])

    def send_chunk(c):
        def send(i, carry):
            t, where = target(i)
            pltpu.make_async_remote_copy(
                src_ref=x.at[c, t], dst_ref=o.at[c, me], send_sem=send_sem.at[c], recv_sem=recv_sem.at[c],
                device_id=where, device_id_type=MESH,
            ).start()
            return carry

        lax.fori_loop(1, 128, send, 0)
        o[c, me] = x[c, me]

    partner = {"rows": 63 - r, "sky": s, "pair": m}
    for c in range(CHUNKS):
        for h in (0, 1):
            for jj in range((8 * h + PAIRS * c) // 2, (8 * h + PAIRS * (c + 1)) // 2):
                second_stage(jj)
        for block in range(128):
            q2, h = block // 2, block % 2
            start = STEP * 2 * (8 * h + PAIRS * c) + q2
            x[c, slot_of(block)] = z[pl.ds(start, LINES, stride=STEP), :]
        if c == 0:
            pl.semaphore_wait(barrier, 129)
        send_chunk(c)
        if c == 0:

            @pl.when(lower)
            def _():
                pltpu.make_async_remote_copy(
                    src_ref=bins.at[pl.ds(32 + 16 * m, 16)], dst_ref=ahead, send_sem=bin_send,
                    recv_sem=bin_recv, device_id=partner, device_id_type=MESH,
                ).start()

            @pl.when(jnp.logical_not(lower))
            def _():
                pltpu.make_async_remote_copy(
                    src_ref=bins.at[pl.ds(48 - 16 * m, 16)], dst_ref=mirror.at[pl.ds(0, 16)],
                    send_sem=bin_send, recv_sem=bin_recv, device_id=partner, device_id_type=MESH,
                ).start()
                beside = lax.rem(64 - r, 32) * (1 - m) + (63 - r) * m
                pltpu.make_async_remote_copy(
                    src_ref=bins.at[pl.ds(48 * m, 8)], dst_ref=mirror.at[pl.ds(16, 8)],
                    send_sem=bin_send, recv_sem=bin_recv,
                    device_id={"rows": beside, "sky": s, "pair": m}, device_id_type=MESH,
                ).start()

    @pl.when(lower)
    def _():
        pltpu.make_async_copy(bins.at[pl.ds(0, 16)], ahead, bin_here).wait()
        pltpu.make_async_copy(bins.at[pl.ds(0, 24)], mirror, bin_recv).wait()
        pltpu.make_async_copy(bins.at[pl.ds(0, 16)], ahead, bin_send).wait()

    @pl.when(jnp.logical_not(lower))
    def _():
        pltpu.make_async_copy(bins.at[pl.ds(0, 24)], mirror, bin_here).wait()
        pltpu.make_async_copy(bins.at[pl.ds(0, 16)], ahead, bin_recv).wait()
        pltpu.make_async_copy(bins.at[pl.ds(0, 24)], mirror, bin_send).wait()

    first_block = (r == 0) & (m == 0)
    none_first = jnp.where(first_block, -1.0, 0.0)
    for src, hi, lo in ((ahead, ahead_hi, ahead_lo), (mirror, mirror_hi, mirror_lo)):
        whole = src[...]
        tiles = [whole[:, 128 * i : 128 * i + 128] for i in range(32)]
        whole = jnp.concatenate(tiles, 0)
        hi[...] = (whole // 32).astype(F32)
        lo[...] = (whole % 32).astype(F32)

    line = lax.broadcasted_iota(jnp.int32, (32, 128), 0)
    lane = lax.broadcasted_iota(jnp.int32, (32, 128), 1)
    p = lane + 128 * line
    signed = jnp.where(p >= SIDE // 2, p - SIDE, p)
    back = jnp.where(p == SIDE // 2, signed, -signed)
    half = lax.broadcasted_iota(jnp.int32, (64, 128), 1) // 64
    block = jnp.where(lower, 4 * r + m, 4 * (63 - r) + 2 + m)
    acc[...] = jnp.zeros_like(acc)

    def spectrum(parts):
        high, low = split(jnp.concatenate([jnp.concatenate(part, 0) for part in parts], 1))
        mid = dot(tah[...], jnp.concatenate([high, low], 0)) + dot(tal[...], high)
        turned = []
        for k in (0, 1):
            re, im = mid[:64, 128 * k : 128 * k + 128], mid[64:, 128 * k : 128 * k + 128]
            re, im = jnp.concatenate([re, re], 0), jnp.concatenate([im, im], 0)
            turned.append(
                jnp.concatenate([re * cwc[...] - im * cws[...], re * cws[...] + im * cwc[...]], 1)
            )
        high, low = split(jnp.concatenate(turned, 0))
        last = dot_nt(tbh[...], high) + dot_nt(tbh[...], low) + dot_nt(tbl[...], high)
        return [
            (last[64 * c : 64 * c + 32, :128], last[64 * c + 32 : 64 * c + 64, :128],
             last[64 * c : 64 * c + 32, 128:], last[64 * c + 32 : 64 * c + 64, 128:])
            for c in (0, 1)
        ]

    def power_of(fields, freq_x, freq_y):
        radius = jnp.maximum(freq_x * freq_x + freq_y * freq_y, 1.0)
        cos_twice = (freq_x * freq_x - freq_y * freq_y) / radius
        sin_twice = 2.0 * freq_x * freq_y / radius
        q_re, q_im, u_re, u_im = fields
        e_re = cos_twice * q_re + sin_twice * u_re
        e_im = cos_twice * q_im + sin_twice * u_im
        b_re = cos_twice * u_re - sin_twice * q_re
        b_im = cos_twice * u_im - sin_twice * q_im
        scale = 1.0 / (SIDE * SIDE)
        terms = (e_re * e_re + e_im * e_im, b_re * b_re + b_im * b_im, e_re * b_re + e_im * b_im)
        return jnp.concatenate([(term * scale).astype(BF) for term in terms], 0)

    def reversed_lines(values):
        turned = dot(values, flip[...])
        parts = [turned[32 * k : 32 * k + 32] for k in range(3)]
        return jnp.concatenate([jnp.where(lane == 0, pltpu.roll(part, 31, 0), part) for part in parts], 0)

    want = lax.broadcasted_iota(jnp.int32, (32, 128), 0).astype(F32).astype(BF)
    wants = (want[:16], want[16:])
    one, none = jnp.ones((16, 128), BF), jnp.zeros((16, 128), BF)

    def add_up(items):
        total = acc[:, 0:32]
        for start in range(0, len(items), UNROLL):
            left, right = [], []
            for kind, c, row, hi, lo in items[start : start + UNROLL]:
                hot, cold = spread(hi(row)), spread(lo(row))
                vals = [spread(powers[kind, c, 32 * k + row : 32 * k + row + 1, :]) for k in range(3)]
                left.append(
                    jnp.concatenate([jnp.where(hot == w, val, none) for val in vals for w in wants], 0)
                )
                right.append(jnp.concatenate([jnp.where(cold == w, one, none) for w in wants], 0))
            total = total + dot_nt(jnp.concatenate(left, 1), jnp.concatenate(right, 1))
        acc[:, 0:32] = total

    def lines_of(ref, index, flipped):
        def get(row):
            at = 31 - row if flipped else row
            return ref[pl.ds(ref.shape[0] // 32 * at + index, 1), :]

        return get

    def pair_of(c, j):
        return [
            [o[c, pl.ds(64 * k, 64), pl.ds(2 * j + ri, 1), :].reshape(64, 128) for ri in (0, 1)] for k in (0, 1)
        ]

    def run_pair(c, j):
        fields = spectrum(pair_of(c, j))
        freq_y = signed.astype(F32)
        items = []
        for k in (0, 1):
            column = 2 * (PAIRS * c + j) + k
            freq_x = (16 * block + column).astype(F32)
            powers[0, k] = power_of(fields[k], freq_x, freq_y).astype(F32)
            powers[1, k] = reversed_lines(power_of(fields[k], -freq_x, back.astype(F32)))
            for row in range(32):
                items.append((0, k, row, lines_of(ahead_hi, column, False), lines_of(ahead_lo, column, False)))
        for k in (0, 1):
            column = 2 * (PAIRS * c + j) + k
            for row in range(32):
                items.append(
                    (1, k, row, lines_of(mirror_hi, 16 - column, True), lines_of(mirror_lo, 16 - column, True))
                )
        add_up(items)

    for c in range(CHUNKS):
        pltpu.make_async_copy(x.at[c, pl.ds(0, 127)], o.at[c, pl.ds(0, 127)], recv_sem.at[c]).wait()
        if c == 0:

            @pl.when(first_block)
            def _():
                parts = []
                for re, im in pair_of(0, 0):
                    parts.append([jnp.where(half == 0, re, pltpu.roll(im, 64, 1)), jnp.zeros((64, 128), F32)])
                fields = spectrum(parts)
                powers[0, 0] = power_of(fields[0], jnp.zeros((32, 128), F32), signed.astype(F32)).astype(F32)
                last = power_of(fields[1], jnp.full((32, 128), -(SIDE // 2) * 1.0, F32), back.astype(F32))
                powers[0, 1] = reversed_lines(last)
                items = [(0, 0, row, lines_of(ahead_hi, 0, False), lines_of(ahead_lo, 0, False)) for row in range(32)]
                items += [
                    (0, 1, row, lines_of(mirror_hi, 16, True), lines_of(mirror_lo, 16, True)) for row in range(32)
                ]
                add_up(items)
                ahead_hi[pl.ds(0, 32, stride=16), :] = jnp.full((32, 128), -1.0, F32)
                mirror_hi[pl.ds(16, 32, stride=24), :] = jnp.full((32, 128), -1.0, F32)

        def body(j, carry):
            run_pair(c, j)
            return carry

        lax.fori_loop(0, PAIRS, body, 0)

    for c in range(CHUNKS):
        pltpu.make_async_copy(x.at[c, pl.ds(0, 127)], o.at[c, pl.ds(0, 127)], send_sem.at[c]).wait()

    wide = lax.broadcasted_iota(jnp.int32, (24, 128), 1) // 32
    part = jnp.zeros((24, 128), F32)
    for u in range(4):
        piece = acc[pl.ds(u, 24, stride=4), :]
        part = jnp.where(wide == u, piece if u == 0 else pltpu.roll(piece, 32 * u, 1), part)
    stage[0] = part
    peers = [[], [], []]
    for i in range(1, 8):
        peers[0].append({"rows": high_row * 8 + lax.rem(low_row + i, 8), "sky": s, "pair": m})
        peers[1].append({"rows": lax.rem(high_row + i, 8) * 8 + low_row, "sky": s, "pair": m})
    for i in range(1, 4):
        other = lax.rem(rep + i, 4)
        peers[2].append({"rows": r, "sky": other // 2, "pair": lax.rem(other, 2)})

    def phase(k, seen, here):
        count = len(peers[k])
        for where in peers[k]:
            pltpu.make_async_remote_copy(
                src_ref=stage.at[k], dst_ref=seen.at[here], send_sem=sum_send.at[k],
                recv_sem=sum_recv.at[k], device_id=where, device_id_type=MESH,
            ).start()
        seen[here] = stage[k]
        some = seen.at[pl.ds(0, count)]
        pltpu.make_async_copy(some, some, sum_send.at[k]).wait()
        pltpu.make_async_copy(some, some, sum_recv.at[k]).wait()

    phase(0, seen_a, low_row)
    stage[1] = jnp.sum(seen_a[...], axis=0)
    phase(1, seen_b, high_row)
    stage[2] = jnp.sum(seen_b[...], axis=0)
    phase(2, seen_c, rep)
    auto = NBINS / (SIDE * SIDE)
    for sky in (0, 1):
        whole = seen_c[2 * sky] + seen_c[2 * sky + 1]
        for k in range(3):
            for i in range(8):
                line_of = whole[8 * k + i : 8 * k + i + 1, :] * (auto if k < 2 else math.sqrt(auto))
                out[k, sky : sky + 1, 128 * i : 128 * i + 128] = line_of


def on_device(maps, mask, bins):
    tables = row_tables() + column_tables()
    here = pl.BlockSpec(memory_space=VMEM)
    there = pl.BlockSpec(memory_space=pl.ANY)
    dma = pltpu.SemaphoreType.DMA
    sums = pl.pallas_call(
        kernel,
        out_shape=jax.ShapeDtypeStruct((3, 2, NBINS), F32),
        in_specs=[here, here, there] + [here] * len(tables),
        out_specs=here,
        scratch_shapes=[
            VMEM((32, 64, 256), BF),
            VMEM((32, 64, 256), BF),
            VMEM((32 * STEP, 128), F32),
            VMEM((CHUNKS, 128, LINES, 128), F32),
            VMEM((CHUNKS, 128, LINES, 128), F32),
            VMEM((16, SIDE), jnp.int32),
            VMEM((24, SIDE), jnp.int32),
            VMEM((16 * 32, 128), F32),
            VMEM((16 * 32, 128), F32),
            VMEM((24 * 32, 128), F32),
            VMEM((24 * 32, 128), F32),
            VMEM((2, 2, 96, 128), F32),
            VMEM((96, 128), F32),
            VMEM((3, 24, 128), F32),
            VMEM((8, 24, 128), F32),
            VMEM((8, 24, 128), F32),
            VMEM((4, 24, 128), F32),
            dma((CHUNKS,)),
            dma((CHUNKS,)),
            dma,
            dma,
            dma,
            dma((3,)),
            dma((3,)),
        ],
        compiler_params=pltpu.CompilerParams(
            collective_id=0, has_side_effects=True, vmem_limit_bytes=48 << 20
        ),
        name="sky_spectra",
    )(maps, mask, bins.T, *tables)
    return jnp.transpose(sums, (1, 0, 2))


def solution(mesh):
    parted = Mesh(mesh.devices.reshape(mesh.shape["rows"], 2, 2), ("rows", "sky", "pair"))
    placed = (P(("sky", "pair"), "rows", None), P("rows", None), P(None, "rows"))
    return jax.shard_map(on_device, mesh=parted, in_specs=placed, out_specs=P(), check_vma=False)
```

time: 113 us -> 83.3 us (0.74)
  Pallas kernels: 96.7 us -> 66.5 us
  local copies, waits for them, and re-layouts: 6.96 us -> 16.1 us
  starting transfers between devices: 9.08 us -> 0 us
    pallas_call x5 -> x1, Pallas kernels: 96.7 us -> 66.5 us  [on_device(): pl.pallas_call(kernel, out_shape=jax.ShapeDtypeStruct((3, 2, NBINS), F32)...]
    unnamed x39 -> x35, local copies, waits for them, and re-layouts: 4.9 us -> 16.1 us
    ppermute x2 -> x0, starting transfers between devices: 9.08 us -> none  [the longest x1 7.66 us: on_device(): other = lax.ppermute(send, 'rows', [(i, 63 - i) for i in range(64)])]
    reshape x3 -> x0, local copies, waits for them, and re-layouts: 2.06 us -> none  [on_device(): return totals(part.reshape(24, 128)).reshape(2, 3, NBINS)]
  transfers between devices with their start and end apart: 2 -> 0, of which waited for: 0 -> 0; matrix products, arithmetic and copies ran while one was open for 0% -> 0% of each run, Pallas kernels for 27% -> 0%
where the time goes in v1:
time: 83.3 us; the launch traced here: 82.6 us
  Pallas kernels  66.5 us (80%)
  local copies, waits for them, and re-layouts  16.1 us (19%)
    pallas_call x1, Pallas kernels, on_device(): pl.pallas_call(kernel, out_shape=jax.ShapeDtypeStruct((3, 2, NBINS), F32)...  66.5 us
    unnamed x35, local copies, waits for them, and re-layouts  16.1 us

profile of v1, /device:TPU:1, one launch (start us, length us, event | category | flops | bytes accessed | tf_op | source)
XLA Modules:
  0.0 82.6 jit_solution(14438983497638516398)
XLA Ops:
  0.0 0.0 copy-start.16
  0.0 0.7 copy-done.16
  0.7 0.0 copy-start
  0.7 1.2 %copy-done = f32[1,64,4096]{2,1,0:T(8,128)S(1)} copy-done((f32[1,64,4096]{2,1,0:T(8,128)S(1)}, f32[1,64,4096]{2,1,0:T(8,128)}, u32[]{:S(2)}) %copy-start) | copy-done | bytes 1048600
  1.9 0.0 copy-start.1
  1.9 1.2 %copy-done.1 = s32[64,4096]{1,0:T(8,128)S(1)} copy-done((s32[64,4096]{1,0:T(8,128)S(1)}, s32[64,4096]{1,0:T(8,128)}, u32[]{:S(2)}) %copy-start.1) | copy-done | bytes 1048600
  3.1 0.0 copy-start.2
  3.2 1.2 %copy-done.2 = s32[4096,64]{0,1:T(8,128)S(1)} copy-done((s32[4096,64]{0,1:T(8,128)S(1)}, s32[4096,64]{0,1:T(8,128)}, u32[]{:S(2)}) %copy-start.2) | copy-done | bytes 1048600
  4.4 0.0 copy-start.3
  4.4 0.9 %copy-done.3 = bf16[512,256]{1,0:T(8,128)(2,1)S(1)} copy-done((bf16[512,256]{1,0:T(8,128)(2,1)S(1)}, bf16[512,256]{1,0:T(8,128)(2,1)}, u32[]{:S(2)}) %copy-start.3) | copy-done | bytes 262168
  5.3 0.0 copy-start.4
  5.3 0.9 %copy-done.4 = bf16[512,256]{1,0:T(8,128)(2,1)S(1)} copy-done((bf16[512,256]{1,0:T(8,128)(2,1)S(1)}, bf16[512,256]{1,0:T(8,128)(2,1)}, u32[]{:S(2)}) %copy-start.4) | copy-done | bytes 262168
  6.3 0.0 copy-start.5
  6.3 0.9 %copy-done.5 = f32[32,8,128]{2,1,0:T(8,128)S(1)} copy-done((f32[32,8,128]{2,1,0:T(8,128)S(1)}, f32[32,8,128]{2,1,0:T(8,128)}, u32[]{:S(2)}) %copy-start.5) | copy-done | bytes 131096
  7.2 0.0 copy-start.6
  7.2 0.9 %copy-done.6 = f32[32,8,128]{2,1,0:T(8,128)S(1)} copy-done((f32[32,8,128]{2,1,0:T(8,128)S(1)}, f32[32,8,128]{2,1,0:T(8,128)}, u32[]{:S(2)}) %copy-start.6) | copy-done | bytes 131096
  8.1 0.0 copy-start.7
  8.1 0.8 %copy-done.7 = bf16[128,256]{1,0:T(8,128)(2,1)S(1)} copy-done((bf16[128,256]{1,0:T(8,128)(2,1)S(1)}, bf16[128,256]{1,0:T(8,128)(2,1)}, u32[]{:S(2)}) %copy-start.7) | copy-done | bytes 65560
  8.9 0.0 copy-start.8
  8.9 0.8 %copy-done.8 = bf16[128,256]{1,0:T(8,128)(2,1)S(1)} copy-done((bf16[128,256]{1,0:T(8,128)(2,1)S(1)}, bf16[128,256]{1,0:T(8,128)(2,1)}, u32[]{:S(2)}) %copy-start.8) | copy-done | bytes 65560
  9.8 0.0 copy-start.9
  9.8 0.8 %copy-done.9 = f32[128,128]{1,0:T(8,128)S(1)} copy-done((f32[128,128]{1,0:T(8,128)S(1)}, f32[128,128]{1,0:T(8,128)}, u32[]{:S(2)}) %copy-start.9) | copy-done | bytes 65560
  10.6 0.0 copy-start.10
  10.6 0.8 %copy-done.10 = f32[128,128]{1,0:T(8,128)S(1)} copy-done((f32[128,128]{1,0:T(8,128)S(1)}, f32[128,128]{1,0:T(8,128)}, u32[]{:S(2)}) %copy-start.10) | copy-done | bytes 65560
  11.4 0.0 copy-start.11
  11.4 0.8 %copy-done.11 = bf16[128,256]{1,0:T(8,128)(2,1)S(1)} copy-done((bf16[128,256]{1,0:T(8,128)(2,1)S(1)}, bf16[128,256]{1,0:T(8,128)(2,1)}, u32[]{:S(2)}) %copy-start.11) | copy-done | bytes 65560
  12.3 0.0 copy-start.12
  12.3 0.8 %copy-done.12 = bf16[128,256]{1,0:T(8,128)(2,1)S(1)} copy-done((bf16[128,256]{1,0:T(8,128)(2,1)S(1)}, bf16[128,256]{1,0:T(8,128)(2,1)}, u32[]{:S(2)}) %copy-start.12) | copy-done | bytes 65560
  13.1 0.0 copy-start.13
  13.1 0.8 %copy-done.13 = bf16[128,256]{1,0:T(8,128)(2,1)S(1)} copy-done((bf16[128,256]{1,0:T(8,128)(2,1)S(1)}, bf16[128,256]{1,0:T(8,128)(2,1)}, u32[]{:S(2)}) %copy-start.13) | copy-done | bytes 65560
  14.0 0.0 copy-start.14
  14.0 0.8 copy-done.14
  14.7 0.0 copy-start.15
  14.7 0.8 copy-done.15
  15.5 66.5 %sky_spectra.1 = f32[3,2,1024]{2,1,0:T(2,128)S(1)} custom-call(f32[1,64,4096]{2,1,0:T(8,128)S(1)} %copy-done, s32[64,4096]{1,0:T(8,128)S(1)} %copy-done.1, s32[64,4096]{1,0:T(8,128)S(1)} %bitcast.2, bf16[512,256]{1,0:T(8,128)(2,1)S(1)} %copy-done.4, bf16[512,256]{1,0:T(8,128)(2,1)S(1)} %copy-done.3, f32[32,8,128]{2,1,0:T(8,128)S(1)} %copy-done.6, ...), custom_call_target="tpu_custom_call" | custom-call | tf_op jit(solution)/shard_map/sky_spectra/pallas_call | solution.py:405
  81.9 0.6 copy.19
Async XLA Ops:
  0.0 0.7 copy-start.16
  0.7 1.2 %copy-start = (f32[1,64,4096]{2,1,0:T(8,128)S(1)}, f32[1,64,4096]{2,1,0:T(8,128)}, u32[]{:S(2)}) copy-start(f32[1,64,4096]{2,1,0:T(8,128)} %maps.1) | copy-start | bytes 3145732
  1.9 1.2 %copy-start.1 = (s32[64,4096]{1,0:T(8,128)S(1)}, s32[64,4096]{1,0:T(8,128)}, u32[]{:S(2)}) copy-start(s32[64,4096]{1,0:T(8,128)} %mask.1) | copy-start | bytes 3145732
  3.1 1.2 %copy-start.2 = (s32[4096,64]{0,1:T(8,128)S(1)}, s32[4096,64]{0,1:T(8,128)}, u32[]{:S(2)}) copy-start(s32[4096,64]{0,1:T(8,128)} %param.19) | copy-start | bytes 3145732
  4.4 0.9 %copy-start.3 = (bf16[512,256]{1,0:T(8,128)(2,1)S(1)}, bf16[512,256]{1,0:T(8,128)(2,1)}, u32[]{:S(2)}) copy-start(bf16[512,256]{1,0:T(8,128)(2,1)} %constant.29.clone.t1l) | copy-start | bytes 786436
  5.3 0.9 %copy-start.4 = (bf16[512,256]{1,0:T(8,128)(2,1)S(1)}, bf16[512,256]{1,0:T(8,128)(2,1)}, u32[]{:S(2)}) copy-start(bf16[512,256]{1,0:T(8,128)(2,1)} %constant.28.clone.t1h) | copy-start | bytes 786436
  6.3 0.9 %copy-start.5 = (f32[32,8,128]{2,1,0:T(8,128)S(1)}, f32[32,8,128]{2,1,0:T(8,128)}, u32[]{:S(2)}) copy-start(f32[32,8,128]{2,1,0:T(8,128)} %constant.31.clone.tws) | copy-start | bytes 393220
  7.2 0.9 %copy-start.6 = (f32[32,8,128]{2,1,0:T(8,128)S(1)}, f32[32,8,128]{2,1,0:T(8,128)}, u32[]{:S(2)}) copy-start(f32[32,8,128]{2,1,0:T(8,128)} %constant.30.clone.twc) | copy-start | bytes 393220
  8.1 0.8 %copy-start.7 = (bf16[128,256]{1,0:T(8,128)(2,1)S(1)}, bf16[128,256]{1,0:T(8,128)(2,1)}, u32[]{:S(2)}) copy-start(bf16[128,256]{1,0:T(8,128)(2,1)} %constant.40.clone.tbl) | copy-start | bytes 196612
  8.9 0.8 %copy-start.8 = (bf16[128,256]{1,0:T(8,128)(2,1)S(1)}, bf16[128,256]{1,0:T(8,128)(2,1)}, u32[]{:S(2)}) copy-start(bf16[128,256]{1,0:T(8,128)(2,1)} %constant.39.clone.tbh) | copy-start | bytes 196612
  9.8 0.8 %copy-start.9 = (f32[128,128]{1,0:T(8,128)S(1)}, f32[128,128]{1,0:T(8,128)}, u32[]{:S(2)}) copy-start(f32[128,128]{1,0:T(8,128)} %constant.38.clone.cws) | copy-start | bytes 196612
  10.6 0.8 %copy-start.10 = (f32[128,128]{1,0:T(8,128)S(1)}, f32[128,128]{1,0:T(8,128)}, u32[]{:S(2)}) copy-start(f32[128,128]{1,0:T(8,128)} %constant.37.clone.cwc) | copy-start | bytes 196612
  11.4 0.8 %copy-start.11 = (bf16[128,256]{1,0:T(8,128)(2,1)S(1)}, bf16[128,256]{1,0:T(8,128)(2,1)}, u32[]{:S(2)}) copy-start(bf16[128,256]{1,0:T(8,128)(2,1)} %constant.35.clone.tah) | copy-start | bytes 196612
  12.3 0.8 %copy-start.12 = (bf16[128,256]{1,0:T(8,128)(2,1)S(1)}, bf16[128,256]{1,0:T(8,128)(2,1)}, u32[]{:S(2)}) copy-start(bf16[128,256]{1,0:T(8,128)(2,1)} %constant.33.clone.t2l) | copy-start | bytes 196612
  13.1 0.8 %copy-start.13 = (bf16[128,256]{1,0:T(8,128)(2,1)S(1)}, bf16[128,256]{1,0:T(8,128)(2,1)}, u32[]{:S(2)}) copy-start(bf16[128,256]{1,0:T(8,128)(2,1)} %constant.32.clone.t2h) | copy-start | bytes 196612
  14.0 0.8 copy-start.14
  14.7 0.8 copy-start.15

commit v2 on v1

--- a/solution.py
+++ b/solution.py
@@ -17,7 +17,7 @@
 F32 = jnp.float32
 VMEM = pltpu.VMEM
 STEP = 72
-CHUNKS = 2
+CHUNKS = 4
 PAIRS = 8 // CHUNKS
 LINES = 2 * PAIRS
 UNROLL = 64
@@ -97,9 +97,24 @@
     return jnp.concatenate([tile, tile], 0).astype(BF)
 
 
-def kernel(
-    maps, mask, bins, t1h, t1l, twc, tws, t2h, t2l, alt, tah, tal, cwc, cws, tbh, tbl, flip,
-    out,
+def kernel(*refs):
+    sources, refs = refs[:16], refs[16:]
+    bins, out, refs = refs[0], refs[1], refs[2:]
+    held, rest = refs[:16], refs[16:]
+    arrived = rest[-1]
+    for i in range(16):
+        pltpu.make_async_copy(sources[i], held[i], arrived.at[i]).start()
+
+    def ready(*places):
+        for i in places:
+            pltpu.make_async_copy(sources[i], held[i], arrived.at[i]).wait()
+
+    work(ready, bins, out, *held, *rest[:-1])
+
+
+def work(
+    ready, bins, out,
+    maps, mask, t1h, t1l, twc, tws, t2h, t2l, alt, tah, tal, cwc, cws, tbh, tbl, flip,
     yh, yl, z, x, o, ahead, mirror, ahead_hi, ahead_lo, mirror_hi, mirror_lo, powers, acc,
     stage, seen_a, seen_b, seen_c, send_sem, recv_sem, bin_send, bin_recv, bin_here, sum_send, sum_recv,
 ):
@@ -128,17 +143,69 @@
 
     @pl.when(lower)
     def _():
-        pltpu.make_async_copy(bins.at[pl.ds(16 * m, 16)], ahead, bin_here).start()
+        pltpu.make_async_copy(bins.at[pl.ds(16 * m, 16)], ahead, bin_here.at[0]).start()
 
     @pl.when(jnp.logical_not(lower))
     def _():
-        pltpu.make_async_copy(bins.at[pl.ds(16 - 16 * m, 16)], mirror.at[pl.ds(0, 16)], bin_here).start()
-        pltpu.make_async_copy(bins.at[pl.ds(32 - 16 * m, 8)], mirror.at[pl.ds(16, 8)], bin_here).start()
-
+        pltpu.make_async_copy(bins.at[pl.ds(16 - 16 * m, 16)], mirror.at[pl.ds(0, 16)], bin_here.at[0]).start()
+        pltpu.make_async_copy(bins.at[pl.ds(32 - 16 * m, 1)], mirror.at[pl.ds(16, 1)], bin_here.at[1]).start()
+
+    partner = {"rows": 63 - r, "sky": s, "pair": m}
+
+    def bins_part(k):
+        def ship(source, count, place, where, sem=k):
+            pltpu.make_async_remote_copy(
+                src_ref=bins.at[pl.ds(source, count)], dst_ref=place, send_sem=bin_send.at[sem],
+                recv_sem=bin_recv.at[sem], device_id=where, device_id_type=MESH,
+            ).start()
+
+        @pl.when(lower)
+        def _():
+            ship(32 + 16 * m + 8 * k, 8, ahead.at[pl.ds(8 * k, 8)], partner)
+
+        @pl.when(jnp.logical_not(lower))
+        def _():
+            ship(56 - 16 * m - 8 * k, 8, mirror.at[pl.ds(8 - 8 * k, 8)], partner)
+            if k == 0:
+                beside = lax.rem(64 - r, 32) * (1 - m) + (63 - r) * m
+                ship(48 * m, 1, mirror.at[pl.ds(16, 1)], {"rows": beside, "sky": s, "pair": m}, 2)
+
+    def bins_ready(k):
+        def wait(count, sem):
+            pltpu.make_async_copy(bins.at[pl.ds(0, count)], mirror.at[pl.ds(0, count)], sem).wait()
+
+        @pl.when(lower)
+        def _():
+            wait(8, bin_recv.at[k])
+            wait(8, bin_send.at[k])
+            if k == 0:
+                wait(16, bin_here.at[0])
+                wait(1, bin_recv.at[2])
+
+        @pl.when(jnp.logical_not(lower))
+        def _():
+            wait(8, bin_recv.at[k])
+            wait(8, bin_send.at[k])
+            if k == 0:
+                wait(16, bin_here.at[0])
+                wait(1, bin_here.at[1])
+                wait(1, bin_send.at[2])
+
+        rows = [(ahead, ahead_hi, ahead_lo, 8 * k, 8), (mirror, mirror_hi, mirror_lo, 8 - 8 * k, 8)]
+        if k == 0:
+            rows.append((mirror, mirror_hi, mirror_lo, 16, 1))
+        for src, hi, lo, start, count in rows:
+            size = src.shape[0]
+            for i in range(32):
+                part = src[start : start + count, 128 * i : 128 * i + 128]
+                hi[size * i + start : size * i + start + count, :] = (part >> 5).astype(F32)
+                lo[size * i + start : size * i + start + count, :] = (part & 31).astype(F32)
+
+    ready(0, 1, 2, 3, 4, 5)
     for g in range(0, 8, 2):
         pair = []
         for k in (g, g + 1):
-            rows = maps[0, 8 * k : 8 * k + 8, :] * mask[8 * k : 8 * k + 8, :].astype(F32)
+            rows = maps[8 * k : 8 * k + 8, :] * mask[8 * k : 8 * k + 8, :].astype(F32)
             pair.append(jnp.concatenate([rows[:, 128 * a : 128 * a + 128] for a in range(32)], 0))
         high, low = split(jnp.concatenate(pair, 1))
         got = dot(t1h[...], high) + dot(t1h[...], low) + dot(t1l[...], high)
@@ -178,7 +245,7 @@
         lax.fori_loop(1, 128, send, 0)
         o[c, me] = x[c, me]
 
-    partner = {"rows": 63 - r, "sky": s, "pair": m}
+    ready(6, 7, 8)
     for c in range(CHUNKS):
         for h in (0, 1):
             for jj in range((8 * h + PAIRS * c) // 2, (8 * h + PAIRS * (c + 1)) // 2):
@@ -189,50 +256,12 @@
             x[c, slot_of(block)] = z[pl.ds(start, LINES, stride=STEP), :]
         if c == 0:
             pl.semaphore_wait(barrier, 129)
+            bins_part(0)
+        if c == CHUNKS // 2:
+            bins_part(1)
         send_chunk(c)
-        if c == 0:
-
-            @pl.when(lower)
-            def _():
-                pltpu.make_async_remote_copy(
-                    src_ref=bins.at[pl.ds(32 + 16 * m, 16)], dst_ref=ahead, send_sem=bin_send,
-                    recv_sem=bin_recv, device_id=partner, device_id_type=MESH,
-                ).start()
-
-            @pl.when(jnp.logical_not(lower))
-            def _():
-                pltpu.make_async_remote_copy(
-                    src_ref=bins.at[pl.ds(48 - 16 * m, 16)], dst_ref=mirror.at[pl.ds(0, 16)],
-                    send_sem=bin_send, recv_sem=bin_recv, device_id=partner, device_id_type=MESH,
-                ).start()
-                beside = lax.rem(64 - r, 32) * (1 - m) + (63 - r) * m
-                pltpu.make_async_remote_copy(
-                    src_ref=bins.at[pl.ds(48 * m, 8)], dst_ref=mirror.at[pl.ds(16, 8)],
-                    send_sem=bin_send, recv_sem=bin_recv,
-                    device_id={"rows": beside, "sky": s, "pair": m}, device_id_type=MESH,
-                ).start()
-
-    @pl.when(lower)
-    def _():
-        pltpu.make_async_copy(bins.at[pl.ds(0, 16)], ahead, bin_here).wait()
-        pltpu.make_async_copy(bins.at[pl.ds(0, 24)], mirror, bin_recv).wait()
-        pltpu.make_async_copy(bins.at[pl.ds(0, 16)], ahead, bin_send).wait()
-
-    @pl.when(jnp.logical_not(lower))
-    def _():
-        pltpu.make_async_copy(bins.at[pl.ds(0, 24)], mirror, bin_here).wait()
-        pltpu.make_async_copy(bins.at[pl.ds(0, 16)], ahead, bin_recv).wait()
-        pltpu.make_async_copy(bins.at[pl.ds(0, 24)], mirror, bin_send).wait()
 
     first_block = (r == 0) & (m == 0)
-    none_first = jnp.where(first_block, -1.0, 0.0)
-    for src, hi, lo in ((ahead, ahead_hi, ahead_lo), (mirror, mirror_hi, mirror_lo)):
-        whole = src[...]
-        tiles = [whole[:, 128 * i : 128 * i + 128] for i in range(32)]
-        whole = jnp.concatenate(tiles, 0)
-        hi[...] = (whole // 32).astype(F32)
-        lo[...] = (whole % 32).astype(F32)
-
     line = lax.broadcasted_iota(jnp.int32, (32, 128), 0)
     lane = lax.broadcasted_iota(jnp.int32, (32, 128), 1)
     p = lane + 128 * line
@@ -241,6 +270,8 @@
     half = lax.broadcasted_iota(jnp.int32, (64, 128), 1) // 64
     block = jnp.where(lower, 4 * r + m, 4 * (63 - r) + 2 + m)
     acc[...] = jnp.zeros_like(acc)
+
+    ready(*range(9, 16))
 
     def spectrum(parts):
         high, low = split(jnp.concatenate([jnp.concatenate(part, 0) for part in parts], 1))
@@ -330,6 +361,7 @@
     for c in range(CHUNKS):
         pltpu.make_async_copy(x.at[c, pl.ds(0, 127)], o.at[c, pl.ds(0, 127)], recv_sem.at[c]).wait()
         if c == 0:
+            bins_ready(0)
 
             @pl.when(first_block)
             def _():
@@ -348,6 +380,9 @@
                 ahead_hi[pl.ds(0, 32, stride=16), :] = jnp.full((32, 128), -1.0, F32)
                 mirror_hi[pl.ds(16, 32, stride=24), :] = jnp.full((32, 128), -1.0, F32)
 
+        if c == CHUNKS // 2:
+            bins_ready(1)
+
         def body(j, carry):
             run_pair(c, j)
             return carry
@@ -399,15 +434,17 @@
 
 def on_device(maps, mask, bins):
     tables = row_tables() + column_tables()
+    loaded = (maps[0], mask) + tables
     here = pl.BlockSpec(memory_space=VMEM)
-    there = pl.BlockSpec(memory_space=pl.ANY)
+    there = pl.BlockSpec(memory_space=pltpu.HBM)
     dma = pltpu.SemaphoreType.DMA
     sums = pl.pallas_call(
         kernel,
         out_shape=jax.ShapeDtypeStruct((3, 2, NBINS), F32),
-        in_specs=[here, here, there] + [here] * len(tables),
+        in_specs=[there] * (3 + len(tables)),
         out_specs=here,
-        scratch_shapes=[
+        scratch_shapes=[VMEM(one.shape, one.dtype) for one in loaded]
+        + [
             VMEM((32, 64, 256), BF),
             VMEM((32, 64, 256), BF),
             VMEM((32 * STEP, 128), F32),
@@ -427,17 +464,18 @@
             VMEM((4, 24, 128), F32),
             dma((CHUNKS,)),
             dma((CHUNKS,)),
-            dma,
-            dma,
-            dma,
             dma((3,)),
             dma((3,)),
+            dma((2,)),
+            dma((3,)),
+            dma((3,)),
+            dma((16,)),
         ],
         compiler_params=pltpu.CompilerParams(
-            collective_id=0, has_side_effects=True, vmem_limit_bytes=48 << 20
+            collective_id=0, has_side_effects=True, vmem_limit_bytes=67043328
         ),
         name="sky_spectra",
-    )(maps, mask, bins.T, *tables)
+    )(*loaded, bins.T)
     return jnp.transpose(sums, (1, 0, 2))
 
 

time: 83.3 us -> 58.7 us (0.70)
  local copies, waits for them, and re-layouts: 16.1 us -> 1.35 us
  Pallas kernels: 66.5 us -> 57.2 us
    unnamed x35 -> x1, local copies, waits for them, and re-layouts: 16.1 us -> 1.35 us
    pallas_call x1, Pallas kernels: 66.5 us -> 57.2 us  [on_device(): pl.pallas_call(kernel, out_shape=jax.ShapeDtypeStruct((3, 2, NBINS), F32)...]
where the time goes in v2:
time: 58.7 us; the launch traced here: 58.6 us
  Pallas kernels  57.2 us (97%)
  local copies, waits for them, and re-layouts  1.35 us (2%)
    pallas_call x1, Pallas kernels, on_device(): pl.pallas_call(kernel, out_shape=jax.ShapeDtypeStruct((3, 2, NBINS), F32)...  57.2 us
    unnamed x1, local copies, waits for them, and re-layouts  1.35 us

profile of v2, /device:TPU:1, one launch (start us, length us, event | category | flops | bytes accessed | tf_op | source)
XLA Modules:
  0.0 58.6 jit_solution(16186494656425859019)
XLA Ops:
  0.0 57.2 %sky_spectra.1 = f32[3,2,1024]{2,1,0:T(2,128)} custom-call(f32[64,4096]{1,0:T(8,128)} %bitcast.3, s32[64,4096]{1,0:T(8,128)} %refs_1_.1, bf16[512,256]{1,0:T(8,128)(2,1)} %constant.28.clone.refs_2_, bf16[512,256]{1,0:T(8,128)(2,1)} %constant.29.clone.refs_3_, f32[32,8,128]{2,1,0:T(8,128)} %constant.30.clone.refs_4_, f32[32,8,128]{2,1,0:T(8,128)} %constant.31.clone.refs_5_, ...), custom_call_target="tpu_custom_call" | custom-call | tf_op jit(solution)/shard_map/sky_spectra/pallas_call | solution.py:441
  57.2 1.3 %copy.19 = f32[2,3,1024]{2,0,1:T(2,128)} copy(f32[2,3,1024]{2,0,1:T(2,128)} %bitcast.5) | data formatting | bytes 49152

commit v3 on v2

--- a/solution.py
+++ b/solution.py
@@ -18,6 +18,8 @@
 VMEM = pltpu.VMEM
 STEP = 72
 CHUNKS = 4
+BIN_AT = (1, 2)
+LIMIT = 32 << 20
 PAIRS = 8 // CHUNKS
 LINES = 2 * PAIRS
 UNROLL = 64
@@ -38,8 +40,8 @@
     stage = np.concatenate([np.cos(first), -np.sin(first)], 0)
     first_high, first_low = halves(np.kron(stage, np.eye(8)))
     turn = angle(np.arange(32), np.arange(128), 4096)
-    turn_cos = np.repeat(np.cos(turn)[:, None, :], 8, 1).astype(np.float32)
-    turn_sin = np.repeat(-np.sin(turn)[:, None, :], 8, 1).astype(np.float32)
+    turn_cos = np.repeat(np.cos(turn), 8, 0).astype(np.float32)
+    turn_sin = np.repeat(-np.sin(turn), 8, 0).astype(np.float32)
     last = angle(np.arange(64), np.arange(128), 128)
     cos, sin = np.cos(last), np.sin(last)
     last_high, last_low = halves(np.block([[cos, sin], [-sin, cos]]))
@@ -98,10 +100,18 @@
 
 
 def kernel(*refs):
-    sources, refs = refs[:16], refs[16:]
-    bins, out, refs = refs[0], refs[1], refs[2:]
+    (maps, mask, bins, narrow, wide, out), refs = refs[:6], refs[6:]
     held, rest = refs[:16], refs[16:]
     arrived = rest[-1]
+    sources = [maps, mask]
+    at = [0, 0]
+    for one in held[2:]:
+        if one.dtype == BF:
+            sources.append(narrow.at[pl.ds(at[0], one.shape[0]), pl.ds(0, one.shape[1])])
+            at[0] += one.shape[0]
+        else:
+            sources.append(wide.at[pl.ds(at[1], one.shape[0])])
+            at[1] += one.shape[0]
     for i in range(16):
         pltpu.make_async_copy(sources[i], held[i], arrived.at[i]).start()
 
@@ -124,18 +134,25 @@
     low_row, high_row = lax.rem(r, 8), r // 8
     rep = 2 * s + m
 
-    def target(i):
-        t = lax.rem(me + i, 128)
-        return t, {"rows": lax.rem(t, 64), "sky": s, "pair": t // 64}
+    def over_sky(action):
+        def other_map(i, carry):
+            action(lax.rem(r + i, 64), 1 - m)
+            return carry
+
+        def same_map(i, carry):
+            action(lax.rem(r + i, 64), m)
+            return carry
+
+        lax.fori_loop(0, 64, other_map, 0)
+        lax.fori_loop(1, 64, same_map, 0)
 
     barrier = pltpu.get_barrier_semaphore()
 
-    def greet(i, carry):
-        _, where = target(i)
+    def greet(row, pair):
+        where = {"rows": row, "sky": s, "pair": pair}
         pl.semaphore_signal(barrier, inc=1, device_id=where, device_id_type=MESH)
-        return carry
-
-    lax.fori_loop(1, 128, greet, 0)
+
+    over_sky(greet)
     for pair in (0, 1):
         pl.semaphore_signal(
             barrier, inc=1, device_id={"rows": r, "sky": 1 - s, "pair": pair}, device_id_type=MESH
@@ -202,6 +219,7 @@
                 lo[size * i + start : size * i + start + count, :] = (part & 31).astype(F32)
 
     ready(0, 1, 2, 3, 4, 5)
+    turn_cos, turn_sin = twc[...].reshape(32, 8, 128), tws[...].reshape(32, 8, 128)
     for g in range(0, 8, 2):
         pair = []
         for k in (g, g + 1):
@@ -213,7 +231,7 @@
         imag = got[256:].reshape(32, 8, 256)
         for k in (0, 1):
             re, im = real[:, :, 128 * k : 128 * k + 128], imag[:, :, 128 * k : 128 * k + 128]
-            pair[k] = (re * twc[...] - im * tws[...], re * tws[...] + im * twc[...])
+            pair[k] = (re * turn_cos - im * turn_sin, re * turn_sin + im * turn_cos)
         for part in (0, 1):
             high, low = split(jnp.concatenate([pair[0][part], pair[1][part]], 1))
             yh[:, 8 * g : 8 * g + 16, 128 * part : 128 * part + 128] = high
@@ -234,15 +252,13 @@
             z[STEP : STEP + 8, :] = jnp.where((row == 0) & (lane < 64), edge[0:8, :128], got[64:72, :128])
 
     def send_chunk(c):
-        def send(i, carry):
-            t, where = target(i)
+        def send(row, pair):
             pltpu.make_async_remote_copy(
-                src_ref=x.at[c, t], dst_ref=o.at[c, me], send_sem=send_sem.at[c], recv_sem=recv_sem.at[c],
-                device_id=where, device_id_type=MESH,
+                src_ref=x.at[c, 64 * pair + row], dst_ref=o.at[c, me], send_sem=send_sem.at[c],
+                recv_sem=recv_sem.at[c], device_id={"rows": row, "sky": s, "pair": pair}, device_id_type=MESH,
             ).start()
-            return carry
-
-        lax.fori_loop(1, 128, send, 0)
+
+        over_sky(send)
         o[c, me] = x[c, me]
 
     ready(6, 7, 8)
@@ -256,9 +272,9 @@
             x[c, slot_of(block)] = z[pl.ds(start, LINES, stride=STEP), :]
         if c == 0:
             pl.semaphore_wait(barrier, 129)
-            bins_part(0)
-        if c == CHUNKS // 2:
-            bins_part(1)
+        for k in (0, 1):
+            if BIN_AT[k] == c:
+                bins_part(k)
         send_chunk(c)
 
     first_block = (r == 0) & (m == 0)
@@ -435,13 +451,15 @@
 def on_device(maps, mask, bins):
     tables = row_tables() + column_tables()
     loaded = (maps[0], mask) + tables
+    narrow = [np.pad(one, ((0, 0), (0, 256 - one.shape[1]))) for one in tables if one.dtype == BF]
+    wide = [one for one in tables if one.dtype != BF]
     here = pl.BlockSpec(memory_space=VMEM)
     there = pl.BlockSpec(memory_space=pltpu.HBM)
     dma = pltpu.SemaphoreType.DMA
     sums = pl.pallas_call(
         kernel,
         out_shape=jax.ShapeDtypeStruct((3, 2, NBINS), F32),
-        in_specs=[there] * (3 + len(tables)),
+        in_specs=[there] * 5,
         out_specs=here,
         scratch_shapes=[VMEM(one.shape, one.dtype) for one in loaded]
         + [
@@ -472,10 +490,10 @@
             dma((16,)),
         ],
         compiler_params=pltpu.CompilerParams(
-            collective_id=0, has_side_effects=True, vmem_limit_bytes=67043328
+            collective_id=0, has_side_effects=True, vmem_limit_bytes=LIMIT
         ),
         name="sky_spectra",
-    )(*loaded, bins.T)
+    )(*[pltpu.with_memory_space_constraint(one, pltpu.HBM) for one in (maps[0], mask, bins.T, jnp.asarray(np.concatenate(narrow, 0)), jnp.asarray(np.concatenate(wide, 0)))])
     return jnp.transpose(sums, (1, 0, 2))
 
 

time: 58.7 us -> 57 us (0.971)
  Pallas kernels: 57.2 us -> 56.4 us
  local copies, waits for them, and re-layouts: 1.35 us -> 0.61 us
    pallas_call x1, Pallas kernels: 57.2 us -> 56.4 us  [on_device(): pl.pallas_call(kernel, out_shape=jax.ShapeDtypeStruct((3, 2, NBINS), F32)...]
    unnamed x1, local copies, waits for them, and re-layouts: 1.35 us -> 0.61 us
where the time goes in v3:
time: 57 us
  Pallas kernels  56.4 us (99%)
  local copies, waits for them, and re-layouts  0.61 us (1%)
    pallas_call x1, Pallas kernels, on_device(): pl.pallas_call(kernel, out_shape=jax.ShapeDtypeStruct((3, 2, NBINS), F32)...  56.4 us

profile of v3, /device:TPU:1, one launch (start us, length us, event | category | flops | bytes accessed | tf_op | source)
XLA Modules:
  0.0 57.0 jit_solution(15663394707750435375)
XLA Ops:
  0.0 56.4 %sky_spectra.1 = f32[3,2,1024]{2,1,0:T(2,128)S(1)} custom-call(f32[64,4096]{1,0:T(8,128)} %bitcast.4, s32[64,4096]{1,0:T(8,128)} %refs_1_.1, s32[64,4096]{1,0:T(8,128)} %bitcast.5, bf16[1936,256]{1,0:T(8,128)(2,1)} %constant.4.clone.refs_3_, f32[768,128]{1,0:T(8,128)} %constant.5.clone.refs_4_), custom_call_target="tpu_custom_call" | custom-call | tf_op jit(solution)/shard_map/sky_spectra/pallas_call | solution.py:459
  56.4 0.6 %copy.7 = f32[2,3,1024]{2,0,1:T(2,128)} copy(f32[2,3,1024]{2,0,1:T(2,128)S(1)} %bitcast.3) | data formatting | bytes 49152
